TPU v7x, 32 devices: a whole 2x2x4 slice. The times are simulated.
32 devices in a mesh: ctx: 8 (over y, x, core), tensor: 4 (over z).
Axes of the slice: x: 2, y: 2, z: 4, core: 2. Of those that a mesh axis runs over, the one named last changes fastest.
Arguments:
- queries: bfloat16 [8192, 4096], P('ctx', 'tensor'), may hold values from -6 to 6
- keys: bfloat16 [8192, 4096], P('ctx', 'tensor'), may hold values from -6 to 6
- values: bfloat16 [8192, 4096], P('ctx', 'tensor'), may hold values from -6 to 6
- doc_ids: int32 [8192], P('ctx'), may hold values from 0 to 7, never falling along the last dimension, each value on 1 to 4096 neighbouring positions
- out_weight: bfloat16 [4096, 6144], P('tensor'), may hold values from -0.125 to 0.125
- grad_out: bfloat16 [8192, 6144], P('ctx', 'tensor'), may hold values from -6 to 6
Outputs:
- attended: bfloat16 [8192, 6144], P('ctx', 'tensor')
- grad_queries: bfloat16 [8192, 4096], P('ctx', 'tensor')
- grad_keys: bfloat16 [8192, 4096], P('ctx', 'tensor')
- grad_values: bfloat16 [8192, 4096], P('ctx', 'tensor')
- grad_weight: float32 [4096, 6144], P('tensor', 'ctx')
Inputs may be any that keep to these rules, and one draw needn't show every extreme that they name: `doc_ids`: never falling along the sequence; each document has 1 to 4096 positions, and one has exactly 4096.
All inputs are finite; a program needn't handle non-finite values.
Results may differ from a plain program's by a relative error of at most 0.015.
Values may be sent and summed in bfloat16 or wider, within the bound.
A program may use at most 192 MiB of HBM per device.

v0:
```python
import jax
import jax.numpy as jnp
from jax import lax
from jax.sharding import PartitionSpec as P

HEAD = 128
careful = lax.Precision.HIGH
epsilon = 1e-06


def prefix(value, axis, combine, identity, reverse):
    length, place = (lax.axis_size(axis), lax.axis_index(axis))
    everything = jax.tree.map(
        lambda part, kind: lax.all_gather(part.astype(kind), axis),
        value,
        (jnp.bfloat16, jnp.bfloat16),
    )
    start = jax.tree.map(
        lambda part, zero: jnp.broadcast_to(jnp.asarray(zero, part.dtype), part.shape),
        value,
        identity,
    )

    def turn(k, before):
        at = length - 1 - k if reverse else k
        reached = at > place if reverse else at < place
        new = combine(
            before, jax.tree.map(lambda part, own: part[at].astype(own.dtype), everything, value)
        )
        return jax.tree.map(lambda a, b: jnp.where(reached, a, b), new, before)

    return lax.fori_loop(0, length, turn, start)


def joined_state(earlier, later):
    earlier_doc, earlier_state = earlier
    later_doc, later_state = later
    vacant = later_doc < 0
    keeping = (earlier_doc == later_doc) | vacant
    doc_result = jnp.where(vacant, earlier_doc, later_doc)
    state_result = later_state + jnp.where(keeping, earlier_state, jnp.zeros_like(earlier_state))
    return (doc_result, state_result)


def carried(doc_cell, state, backward):
    identity = (jnp.full((1, 1, 1), -1.0, jnp.float32), jnp.zeros_like(state))
    if backward:
        doc_in, state_in = prefix((doc_cell, state), "ctx", joined_state, identity, True)
    else:
        doc_in, state_in = prefix((doc_cell, state), "ctx", joined_state, identity, False)
    return (doc_in.reshape(()), state_in)


def body(queries, keys, values, doc_ids, out_weight, grad_out):
    rows = queries.shape[0]
    head_size = HEAD
    heads_here = queries.shape[1] // head_size
    query_rows = queries.reshape(rows, heads_here, head_size)
    key_rows = keys.reshape(rows, heads_here, head_size)
    value_rows = values.reshape(rows, heads_here, head_size)
    doc_float = doc_ids.astype(jnp.float32)
    order = jnp.arange(rows)
    mask = ((order[:, None] >= order[None, :]) & (doc_float[:, None] == doc_float[None, :])).astype(
        jnp.float32
    )
    scores = (
        jnp.einsum("the,uhe->htu", query_rows, key_rows, preferred_element_type=jnp.float32)
        * mask[None]
    )
    local = jnp.einsum(
        "htu,uhf->thf", scores, value_rows, precision=careful, preferred_element_type=jnp.float32
    )
    tail_mask = (doc_float == doc_float[-1]).astype(jnp.bfloat16)[:, None, None]
    tail_state = jnp.einsum(
        "uhe,uhf->hef", key_rows * tail_mask, value_rows, preferred_element_type=jnp.float32
    )
    last_doc, state_in = carried(doc_float[-1].reshape(1, 1, 1), tail_state, False)
    joined = (doc_float == last_doc).astype(jnp.float32)[:, None, None]
    opened = local + joined * jnp.einsum(
        "the,hef->thf", query_rows, state_in, precision=careful, preferred_element_type=jnp.float32
    )
    inverse = lax.rsqrt(jnp.mean(opened * opened, axis=-1, keepdims=True) + epsilon)
    normed = opened * inverse
    normed_low = normed.reshape(rows, heads_here * head_size).astype(jnp.bfloat16)
    partial_out = jnp.dot(normed_low, out_weight, preferred_element_type=jnp.float32)
    attended = lax.psum_scatter(
        partial_out.astype(jnp.bfloat16), "tensor", scatter_dimension=1, tiled=True
    )
    grad_whole = lax.all_gather(grad_out, "tensor", axis=1, tiled=True)
    grad_normed = lax.dot_general(
        grad_whole, out_weight, (((1,), (1,)), ((), ())), preferred_element_type=jnp.float32
    )
    weight_term = lax.dot_general(
        normed_low, grad_whole, (((0,), (0,)), ((), ())), preferred_element_type=jnp.float32
    )
    grad_weight = lax.psum_scatter(
        weight_term.astype(jnp.bfloat16), "ctx", scatter_dimension=1, tiled=True
    ).astype(jnp.float32)
    grad_normed = grad_normed.reshape(rows, heads_here, head_size)
    grad_opened = inverse * (
        grad_normed - normed * jnp.mean(grad_normed * normed, axis=-1, keepdims=True)
    )
    head_mask = (doc_float == doc_float[0]).astype(jnp.bfloat16)[:, None, None]
    head_state = jnp.einsum(
        "the,thf->hef",
        query_rows * head_mask,
        grad_opened,
        precision=careful,
        preferred_element_type=jnp.float32,
    )
    first_doc, state_back = carried(doc_float[0].reshape(1, 1, 1), head_state, True)
    starts = (doc_float == first_doc).astype(jnp.float32)[:, None, None]
    grad_scores = (
        jnp.einsum(
            "thf,uhf->htu",
            grad_opened,
            value_rows,
            precision=careful,
            preferred_element_type=jnp.float32,
        )
        * mask[None]
    )
    grad_query = jnp.einsum(
        "htu,uhe->the", grad_scores, key_rows, precision=careful, preferred_element_type=jnp.float32
    ) + joined * jnp.einsum(
        "thf,hef->the", grad_opened, state_in, precision=careful, preferred_element_type=jnp.float32
    )
    grad_key = jnp.einsum(
        "htu,the->uhe",
        grad_scores,
        query_rows,
        precision=careful,
        preferred_element_type=jnp.float32,
    ) + starts * jnp.einsum(
        "uhf,hef->uhe",
        value_rows,
        state_back,
        precision=careful,
        preferred_element_type=jnp.float32,
    )
    grad_value = jnp.einsum(
        "htu,thf->uhf", scores, grad_opened, precision=careful, preferred_element_type=jnp.float32
    ) + starts * jnp.einsum(
        "uhe,hef->uhf", key_rows, state_back, precision=careful, preferred_element_type=jnp.float32
    )
    flat = heads_here * head_size
    return (
        attended,
        grad_query.reshape(rows, flat).astype(jnp.bfloat16),
        grad_key.reshape(rows, flat).astype(jnp.bfloat16),
        grad_value.reshape(rows, flat).astype(jnp.bfloat16),
        grad_weight,
    )


def solution(mesh):
    return jax.shard_map(
        body,
        mesh=mesh,
        in_specs=(
            P("ctx", "tensor"),
            P("ctx", "tensor"),
            P("ctx", "tensor"),
            P("ctx"),
            P("tensor", None),
            P("ctx", "tensor"),
        ),
        out_specs=(
            P("ctx", "tensor"),
            P("ctx", "tensor"),
            P("ctx", "tensor"),
            P("ctx", "tensor"),
            P("tensor", "ctx"),
        ),
        check_vma=False,
    )
```

profile of v0, /device:TPU:0, one launch (start us, length us, event | category | flops | bytes accessed | tf_op | source)
XLA Modules:
  0.0 642.6 jit_solution(15173689273183936138)
XLA Ops:
  8.6 3.6 copy.65
  12.2 4.1 copy.36
  16.3 1.3 compare_convert_fusion.1
  17.6 3.1 fusion.46
  22.7 1.4 dynamic-update-slice
  24.1 1.4 dynamic-update-slice.1
  25.5 15.8 %all-reduce.2 = (bf16[8]{0:T(256)(128)(2,1)S(1)}, bf16[8]{0:T(256)(128)(2,1)}) all-reduce(bf16[8]{0:T(256)(128)(2,1)S(1)} %dynamic-update-slice, bf16[8]{0:T(256)(128)(2,1)S(1)} %dynamic-update-slice.1), channel_id=2, replica_groups=mesh['ctx'=8,'tensor'=4] {'ctx'}, use_global_device_ids=true, to_apply=%add | all-reduce | flops 16 | bytes 64
  41.3 4.0 copy.62
  45.3 2.8 fusion.17
  49.1 14.8 %fusion.32 = f32[8,1024,1024]{2,1,0:T(8,128)} fusion(bf16[1024,8,128]{0,2,1:T(8,128)(2,1)S(1)} %bitcast.128, bf16[1024,1024]{1,0:T(8,128)(2,1)S(1)} %copy-done.7), kind=kOutput, calls=%fused_computation.41 | convolution fusion | flops 2147483648 | bytes 37748736 | tf_op jit(solution)/shard_map/the,uhe->htu/dot_general | solution.py:67
  63.9 31.0 %while.34 = (s32[]{:T(128)}, f32[1,1,1]{2,1,0:T(1,128)}, f32[8,128,128]{2,1,0:T(8,128)S(1)}, s32[]{:T(128)}, bf16[8,1,1,1]{0,3,2,1:T(2,128)(2,1)S(1)}, /*index=5...) while((s32[]{:T(128)}, f32[1,1,1]{2,1,0:T(1,128)}, ...), condition=%wide.region_1.2_spmd.clone, body=%wide.region_0.1_spmd.clone.sunk | while | flops 655369 | bytes 1310887 | solution.py:32
  65.8 1.3 fusion.83
  69.7 1.3 fusion.83
  73.6 1.3 fusion.83
  77.5 1.3 fusion.83
  81.4 1.3 fusion.83
  89.1 1.3 fusion.83
  93.0 1.3 fusion.83
  94.9 4.9 fusion.55
  99.8 21.0 %multiply_reduce_fusion.1 = (f32[1024,8]{0,1:T(8,128)S(1)}, f32[1024,8,128]{0,2,1:T(8,128)}) fusion(f32[8,128,1024]{2,1,0:T(8,128)} %fusion.55, f32[1024]{0:T(1024)S(1)} %compare_convert_fusion.2, f32[8,1024,1024]{2,1,0:T(8,128)} %fusion.32, f32[1024,1024]{1,0:T(8,128)} %fusion.17, bf16[1024,1024]{1,0:T(8,128)(2,1)S(1)} %copy-done), kind=kOutput, calls=%fused_computation.28 | convolution fusion | flops 6455025664 | bytes 48271360 | tf_op jit(solution)/shard_map/htu,uhf->thf/dot_general | solution.py:70
  120.8 150.5 %all-gather.8.cloned.1.call-done = bf16[1024,6144]{1,0:T(8,128)(2,1)} async-done(((bf16[1024,1536]{1,0:T(8,128)(2,1)}), bf16[1024,6144]{1,0:T(8,128)(2,1)}) %all-gather.8.cloned.1.call-update) | async-done | bytes 12582928 | tf_op jit(solution)/shard_map/all_gather | solution.py:89
  271.3 21.3 %multiply_reduce_fusion = (f32[1024,8]{0,1:T(8,128)S(1)}, f32[1024,1024]{0,1:T(8,128)S(1)}) fusion(f32[1024,8,128]{0,2,1:T(8,128)} %get-tuple-element.385, f32[1024,8]{0,1:T(8,128)S(1)} %add_rsqrt_fusion, bf16[1024,6144]{1,0:T(8,128)(2,1)} %all-gather.8.cloned.1.call-done, bf16[1024,6144]{1,0:T(8,128)(2,1)} %param.14), kind=kOutput, calls=%fused_computation.27 | convolution fusion | flops 12888039424 | bytes 33619968 | tf_op jit(solution)/shard_map/dot_general | solution.py:90
  292.7 3.0 subtract_multiply_fusion
  295.6 2.0 copy-done.3
  297.6 2.1 fusion.43
  299.7 20.9 %convolution_convert_fusion = bf16[1024,6144]{1,0:T(8,128)(2,1)} fusion(bf16[1024,1024]{0,1:T(8,128)(2,1)} %bitcast.136, bf16[1024,6144]{1,0:T(8,128)(2,1)} %all-gather.8.cloned.1.call-done), kind=kOutput, calls=%fused_computation.18 | convolution fusion | flops 12891193344 | bytes 27262976 | tf_op jit(solution)/shard_map/dot_general | solution.py:93
  320.7 22.6 %convolution_convert_fusion.1 = bf16[1024,6144]{1,0:T(8,128)(2,1)} fusion(bf16[1024,1024]{0,1:T(8,128)(2,1)} %bitcast.137, bf16[1024,6144]{1,0:T(8,128)(2,1)} %param.14), kind=kOutput, calls=%fused_computation.19 | convolution fusion | flops 12891193344 | bytes 27262976 | tf_op jit(solution)/shard_map/dot_general | solution.py:85
  343.4 7.2 %fusion.56 = f32[8,128,1024]{2,1,0:T(8,128)} fusion(f32[8,128,128]{2,1,0:T(8,128)S(1)} %get-tuple-element.271, f32[1024,8,128]{0,2,1:T(8,128)} %copy-done.3), kind=kOutput, calls=%fused_computation.67 | convolution fusion | flops 805306368 | bytes 8912896 | tf_op jit(solution)/shard_map/thf,hef->the/dot_general | solution.py:125
  350.6 18.5 %fusion.27 = f32[8,1024,1024]{2,1,0:T(8,128)} fusion(f32[1024,8,128]{0,2,1:T(8,128)} %copy-done.3, bf16[1024,1024]{1,0:T(8,128)(2,1)S(1)} %copy-done), kind=kOutput, calls=%fused_computation.36 | convolution fusion | flops 6442450944 | bytes 39845888 | tf_op jit(solution)/shard_map/thf,uhf->htu/dot_general | solution.py:114
  369.2 19.0 %fusion.15 = bf16[1024,8,128]{0,2,1:T(8,128)(2,1)} fusion(f32[8,128,1024]{2,1,0:T(8,128)} %fusion.56, bf16[1024,8,128]{0,2,1:T(8,128)(2,1)} %copy.36, f32[8,1024,1024]{2,1,0:T(8,128)} %fusion.27, f32[1024,1024]{1,0:T(8,128)S(1)} %copy-done.1, f32[1024]{0:T(1024)S(1)} %compare_convert_fusion.2), kind=kOutput, calls=%fused_computation.23 | convolution fusion | flops 6453985280 | bytes 46141440 | tf_op jit(solution)/shard_map/htu,uhe->the/dot_general | solution.py:123
  388.1 3.9 copy.52
  392.1 19.4 %fusion.6 = f32[8,128,1024]{2,1,0:T(8,128)} fusion(f32[1024,8,128]{0,2,1:T(8,128)} %copy-done.3, f32[8,1024,1024]{2,1,0:T(8,128)} %fusion.32, f32[1024,1024]{1,0:T(8,128)} %fusion.17), kind=kOutput, calls=%fused_computation.10 | convolution fusion | flops 6450839552 | bytes 46137344 | tf_op jit(solution)/shard_map/htu,thf->uhf/dot_general | solution.py:141
  411.4 31.1 %while.35 = (s32[]{:T(128)}, f32[1,1,1]{2,1,0:T(1,128)}, f32[8,128,128]{2,1,0:T(8,128)S(1)}, s32[]{:T(128)}, bf16[8,1,1,1]{0,3,2,1:T(2,128)(2,1)S(1)}, /*index=5...) while((s32[]{:T(128)}, f32[1,1,1]{2,1,0:T(1,128)}, ...), condition=%wide.region_6.7_spmd.clone, body=%wide.region_5.6_spmd.clone.sunk | while | flops 655373 | bytes 1310949 | solution.py:32
  413.4 1.3 fusion.84
  417.2 1.3 fusion.84
  421.1 1.3 fusion.84
  424.9 1.3 fusion.84
  428.8 1.3 fusion.84
  432.7 1.3 fusion.84
  436.6 1.3 fusion.84
  440.4 1.3 fusion.84
  442.5 5.7 add_convert_fusion
  448.2 3.9 copy.54
  452.2 1.3 fusion.25
  455.0 17.1 %fusion.14 = bf16[1024,8,128]{0,2,1:T(8,128)(2,1)} fusion(f32[8,128,1024]{2,1,0:T(8,128)S(1)} %fusion.25, bf16[1024,8,128]{0,2,1:T(8,128)(2,1)S(1)} %bitcast.130, f32[8,1024,1024]{2,1,0:T(8,128)} %fusion.27, f32[1024,1024]{1,0:T(8,128)S(1)} %copy-done.2, f32[1024]{0:T(1024)S(1)} %compare_convert_fusion), kind=kOutput, calls=%fused_computation.21 | convolution fusion | flops 6453985280 | bytes 46141440 | tf_op jit(solution)/shard_map/htu,the->uhe/dot_general | solution.py:128
  472.1 4.0 copy.53
  476.1 3.3 convert_element_type.139
  479.4 156.5 %reduce-scatter.3.cloned.1.call-done = bf16[1024,1536]{1,0:T(8,128)(2,1)} async-done(((bf16[1024,6144]{1,0:T(8,128)(2,1)}), bf16[1024,1536]{1,0:T(8,128)(2,1)}) %reduce-scatter.3.cloned.1.call-update) | async-done | bytes 3145744 | tf_op jit(solution)/shard_map/reduce_scatter | solution.py:86
  (69 shorter events, 17.4 us)
Async XLA Ops:
  7.2 10.4 %copy-start = (bf16[1024,1024]{1,0:T(8,128)(2,1)S(1)}, bf16[1024,1024]{1,0:T(8,128)(2,1)}, u32[]{:S(2)}) copy-start(bf16[1024,1024]{1,0:T(8,128)(2,1)} %param.12) | copy-start | bytes 6291460
  7.2 56.7 %all-gather.10.cloned.1.call-start = ((), (), s32[]{:S(2)}) async-start(), calls=%async_computation.5 | async-start | bytes 2359296 | tf_op jit(solution)/shard_map/all_gather | solution.py:14
  8.6 7.7 %copy-start.10 = (s32[1024]{0:T(1024)S(1)}, s32[1024]{0:T(1024)}, u32[]{:S(2)}) copy-start(s32[1024]{0:T(1024)} %param.13) | copy-start | bytes 12292
  17.6 3.9 copy-start.13
  20.7 250.5 %all-gather.8.cloned.1.call-start = ((), (), s32[]{:S(2)}) async-start(), calls=%async_computation.3 | async-start | bytes 15728640 | tf_op jit(solution)/shard_map/all_gather | solution.py:89
  21.5 389.9 %all-gather.12.cloned.1.call-start = ((), (), s32[]{:S(2)}) async-start(), calls=%async_computation.6 | async-start | bytes 2359296 | tf_op jit(solution)/shard_map/all_gather | solution.py:14
  45.3 2.8 copy-start.4
  45.3 3.8 copy-start.7
  271.3 21.3 %copy-start.8 = (f32[1024,8,128]{0,2,1:T(8,128)S(1)}, f32[1024,8,128]{0,2,1:T(8,128)}, u32[]{:S(2)}) copy-start(f32[1024,8,128]{0,2,1:T(8,128)} %get-tuple-element.385) | copy-start | bytes 12582916
  292.6 5.0 copy-start.5
  295.6 2.0 copy-start.3
  299.7 176.4 %reduce-scatter.5.cloned.1.call-start = ((), (), s32[]{:S(2)}) async-start(), calls=%async_computation.4 | async-start | bytes 14155776 | tf_op jit(solution)/shard_map/reduce_scatter | solution.py:96
  320.7 315.2 %reduce-scatter.3.cloned.1.call-start = ((), (), s32[]{:S(2)}) async-start(), calls=%async_computation.2 | async-start | bytes 15728640 | tf_op jit(solution)/shard_map/reduce_scatter | solution.py:86
  350.6 18.5 %copy-start.1 = (f32[1024,1024]{1,0:T(8,128)S(1)}, f32[1024,1024]{1,0:T(8,128)}, u32[]{:S(2)}) copy-start(f32[1024,1024]{1,0:T(8,128)} %fusion.17) | copy-start | bytes 12582916
  392.1 19.4 %copy-start.9 = (f32[8,128,128]{2,1,0:T(8,128)S(1)}, f32[8,128,128]{2,1,0:T(8,128)}, u32[]{:S(2)}) copy-start(f32[8,128,128]{2,1,0:T(8,128)} %custom-call.1) | copy-start | bytes 1572868
  392.1 19.4 %copy-start.12 = (bf16[8]{0:T(256)(128)(2,1)S(1)}, bf16[8]{0:T(256)(128)(2,1)}, u32[]{:S(2)}) copy-start(bf16[8]{0:T(256)(128)(2,1)} %get-tuple-element.375) | copy-start | bytes 52
  411.4 31.1 %copy-start.11 = (s32[1024]{0:T(1024)S(1)}, s32[1024]{0:T(1024)}, u32[]{:S(2)}) copy-start(s32[1024]{0:T(1024)} %param.13) | copy-start | bytes 12292
  452.2 2.2 copy-start.2
  452.2 2.9 copy-start.6
Sparse Core Ops, SparseCore 0:
  20.9 30.5 all-gather.9
  53.1 218.1 all-gather.7
  299.8 25.9 all-gather.11
  329.2 91.9 reduce-scatter.4
  423.9 211.8 reduce-scatter.2
where the time goes:
time: 652 us; the launch traced here: 643 us
  waiting for transfers between devices  308 us (47%)
  matrix products  199 us (31%)
  local copies, waits for them, and re-layouts  42.5 us (7%)
  loops' own time  31.9 us (5%)
  other arithmetic  31.5 us (5%)
  blocking collectives  15.8 us (2%)
  between operations  14.1 us (2%)
    reduce_scatter x1, waiting for transfers between devices, body(): lax.psum_scatter(partial_out.astype(jnp.bfloat16), 'tensor', scatter_dime...  156 us
    all_gather x1, waiting for transfers between devices, body(): grad_whole = lax.all_gather(grad_out, 'tensor', axis=1, tiled=True)  150 us
    another operation x2, loops' own time, prefix(): return lax.fori_loop(0, length, turn, start)  31.9 us
    unnamed x37, local copies, waits for them, and re-layouts  23.4 us
    dot_general x1, matrix products, body(): jnp.dot(normed_low, out_weight, preferred_element_type=jnp.float32)  22.6 us
    dot_general x1, matrix products, body(): lax.dot_general(grad_whole, out_weight, (((1,), (1,)), ((), ())), preferr...  21.3 us
    dot_general x1, matrix products, body(): jnp.einsum('htu,uhf->thf', scores, value_rows, precision=careful, preferr...  21 us
    dot_general x1, matrix products, body(): lax.dot_general(normed_low, grad_whole, (((0,), (0,)), ((), ())), preferr...  20.9 us
  transfers between devices with their start and end apart: 5, of which 2 were waited for; matrix products, arithmetic and copies ran while one was open for 36% of the time, Pallas kernels for 0%

commit v1 on v0

--- a/solution.py
+++ b/solution.py
@@ -6,6 +6,11 @@
 HEAD = 128
 careful = lax.Precision.HIGH
 epsilon = 1e-06
+
+
+def cut_zones_for(v0):
+    b_now = jnp.concatenate(lax.all_gather(v0, "tensor"), 1)
+    return b_now
 
 
 def prefix(value, axis, combine, identity, reverse):
@@ -86,7 +91,7 @@
     attended = lax.psum_scatter(
         partial_out.astype(jnp.bfloat16), "tensor", scatter_dimension=1, tiled=True
     )
-    grad_whole = lax.all_gather(grad_out, "tensor", axis=1, tiled=True)
+    grad_whole = cut_zones_for(grad_out)
     grad_normed = lax.dot_general(
         grad_whole, out_weight, (((1,), (1,)), ((), ())), preferred_element_type=jnp.float32
     )

time: 652 us -> 691 us (1.060)
  local copies, waits for them, and re-layouts: 42.5 us -> 96.3 us
  waiting for transfers between devices: 308 us -> 299 us
    reshape x0 -> x1, local copies, waits for them, and re-layouts: none -> 23.7 us  [cut_zones_for(): b_now = jnp.concatenate(lax.all_gather(v0, 'tensor'), 1)]
    all_gather x0 -> x1, local copies, waits for them, and re-layouts: none -> 17.3 us  [cut_zones_for(): b_now = jnp.concatenate(lax.all_gather(v0, 'tensor'), 1)]
    unnamed x37 -> x40, local copies, waits for them, and re-layouts: 23.4 us -> 36.5 us
    reduce_scatter x1, waiting for transfers between devices: 156 us -> 148 us  [body(): lax.psum_scatter(partial_out.astype(jnp.bfloat16), 'tensor', scatter_dime...]
  transfers between devices with their start and end apart: 5 -> 5, of which waited for: 2 -> 2; matrix products, arithmetic and copies ran while one was open for 36% -> 35% of each run, Pallas kernels for 0% -> 0%
where the time goes in v1:
time: 691 us; the launch traced here: 686 us
  waiting for transfers between devices  299 us (43%)
  matrix products  197 us (29%)
  local copies, waits for them, and re-layouts  96.3 us (14%)
  other arithmetic  31.5 us (5%)
  loops' own time  31.3 us (5%)
  blocking collectives  16.3 us (2%)
  between operations  14.1 us (2%)
    all_gather x1, waiting for transfers between devices, cut_zones_for(): b_now = jnp.concatenate(lax.all_gather(v0, 'tensor'), 1)  151 us
    reduce_scatter x1, waiting for transfers between devices, body(): lax.psum_scatter(partial_out.astype(jnp.bfloat16), 'tensor', scatter_dime...  148 us
    unnamed x40, local copies, waits for them, and re-layouts  36.5 us
    another operation x2, loops' own time, prefix(): return lax.fori_loop(0, length, turn, start)  31.3 us
    reshape x1, local copies, waits for them, and re-layouts, cut_zones_for(): b_now = jnp.concatenate(lax.all_gather(v0, 'tensor'), 1)  23.7 us
    dot_general x1, matrix products, body(): jnp.dot(normed_low, out_weight, preferred_element_type=jnp.float32)  22.3 us
    dot_general x1, matrix products, body(): lax.dot_general(grad_whole, out_weight, (((1,), (1,)), ((), ())), preferr...  21.5 us
    dot_general x1, matrix products, body(): jnp.einsum('htu,uhf->thf', scores, value_rows, precision=careful, preferr...  21.1 us
  transfers between devices with their start and end apart: 5, of which 2 were waited for; matrix products, arithmetic and copies ran while one was open for 35% of the time, Pallas kernels for 0%

profile of v1, /device:TPU:0, one launch (start us, length us, event | category | flops | bytes accessed | tf_op | source)
XLA Modules:
  0.0 686.0 jit_solution(15018766384384274481)
XLA Ops:
  8.6 3.6 copy.67
  12.2 4.1 copy.37
  16.3 1.3 compare_convert_fusion.1
  17.6 3.1 fusion.46
  22.7 1.4 dynamic-update-slice
  24.1 1.4 dynamic-update-slice.1
  25.5 16.3 %all-reduce.2 = (bf16[8]{0:T(256)(128)(2,1)S(1)}, bf16[8]{0:T(256)(128)(2,1)}) all-reduce(bf16[8]{0:T(256)(128)(2,1)S(1)} %dynamic-update-slice, bf16[8]{0:T(256)(128)(2,1)S(1)} %dynamic-update-slice.1), channel_id=2, replica_groups=mesh['ctx'=8,'tensor'=4] {'ctx'}, use_global_device_ids=true, to_apply=%add | all-reduce | flops 16 | bytes 64
  41.9 4.0 copy.64
  45.8 2.8 fusion.17
  49.6 15.0 %fusion.32 = f32[8,1024,1024]{2,1,0:T(8,128)} fusion(bf16[1024,8,128]{0,2,1:T(8,128)(2,1)S(1)} %bitcast.133, bf16[1024,1024]{1,0:T(8,128)(2,1)S(1)} %copy-done.7), kind=kOutput, calls=%fused_computation.41 | convolution fusion | flops 2147483648 | bytes 37748736 | tf_op jit(solution)/shard_map/the,uhe->htu/dot_general | solution.py:72
  64.6 30.2 %while.34 = (s32[]{:T(128)}, f32[1,1,1]{2,1,0:T(1,128)}, f32[8,128,128]{2,1,0:T(8,128)S(1)}, s32[]{:T(128)}, bf16[8,1,1,1]{0,3,2,1:T(2,128)(2,1)S(1)}, /*index=5...) while((s32[]{:T(128)}, f32[1,1,1]{2,1,0:T(1,128)}, ...), condition=%wide.region_1.2_spmd.clone, body=%wide.region_0.1_spmd.clone.sunk | while | flops 655369 | bytes 1310887 | solution.py:37
  66.4 1.3 fusion.84
  77.8 1.3 fusion.84
  89.1 1.3 fusion.84
  92.8 1.3 fusion.84
  94.8 4.9 fusion.56
  99.7 21.1 %multiply_reduce_fusion.1 = (f32[1024,8]{0,1:T(8,128)S(1)}, f32[1024,8,128]{0,2,1:T(8,128)}) fusion(f32[8,128,1024]{2,1,0:T(8,128)} %fusion.56, f32[1024]{0:T(1024)S(1)} %compare_convert_fusion.2, f32[8,1024,1024]{2,1,0:T(8,128)} %fusion.32, f32[1024,1024]{1,0:T(8,128)} %fusion.17, bf16[1024,1024]{1,0:T(8,128)(2,1)S(1)} %copy-done), kind=kOutput, calls=%fused_computation.28 | convolution fusion | flops 6455025664 | bytes 48271360 | tf_op jit(solution)/shard_map/htu,uhf->thf/dot_general | solution.py:75
  120.7 150.6 %all-gather.11.cloned.1.call-done = bf16[4096,1536]{1,0:T(8,128)(2,1)} async-done(((bf16[1024,1536]{1,0:T(8,128)(2,1)}), bf16[4096,1536]{1,0:T(8,128)(2,1)}) %all-gather.11.cloned.1.call-update) | async-done | bytes 12582928 | tf_op jit(solution)/shard_map/all_gather | solution.py:12
  271.3 17.3 %copy.99 = bf16[4,1024,1536]{2,0,1:T(4,128)(2,1)} copy(bf16[4,1024,1536]{2,1,0:T(8,128)(2,1)} %bitcast.137) | data formatting | bytes 25165824 | tf_op jit(solution)/shard_map/all_gather | solution.py:12
  288.6 23.7 %reshape.150 = bf16[1024,6144,1]{1,0,2:T(8,128)(2,1)} reshape(bf16[1024,4,1536]{2,1,0:T(4,128)(2,1)} %bitcast.130) | data formatting | bytes 25165824 | tf_op jit(solution)/shard_map/reshape | solution.py:12
  312.3 21.5 %multiply_reduce_fusion = (f32[1024,8]{0,1:T(8,128)S(1)}, f32[1024,8,128]{0,2,1:T(8,128)S(1)}) fusion(f32[1024,8,128]{0,2,1:T(8,128)} %get-tuple-element.387, f32[1024,8]{0,1:T(8,128)S(1)} %add_rsqrt_fusion, bf16[1024,6144,1]{1,0,2:T(8,128)(2,1)} %reshape.150, bf16[8,128,6144]{2,1,0:T(8,128)(2,1)} %bitcast.147), kind=kOutput, calls=%fused_computation.27 | convolution fusion | flops 12888039424 | bytes 33619968 | tf_op jit(solution)/shard_map/dot_general | solution.py:95
  333.8 3.0 subtract_multiply_fusion
  336.8 2.0 copy-done.3
  338.7 2.1 fusion.43
  340.9 13.1 %copy.68 = bf16[128,8,4,1536]{3,1,2,0:T(8,128)(2,1)} copy(bf16[128,8,4,1536]{3,2,1,0:T(4,128)(2,1)} %bitcast.131) | data formatting | bytes 25165824
  354.0 20.3 %convolution_convert_fusion = bf16[1024,6144]{1,0:T(8,128)(2,1)} fusion(bf16[1024,1024]{0,1:T(8,128)(2,1)S(1)} %bitcast.144, bf16[1024,6144]{1,0:T(8,128)(2,1)} %bitcast.138), kind=kOutput, calls=%fused_computation.18 | convolution fusion | flops 12891193344 | bytes 27262976 | tf_op jit(solution)/shard_map/dot_general | solution.py:98
  374.4 22.3 %convolution_convert_fusion.1 = bf16[1024,6144]{1,0:T(8,128)(2,1)} fusion(bf16[1024,1024]{0,1:T(8,128)(2,1)} %bitcast.143, bf16[1024,6144]{1,0:T(8,128)(2,1)} %param.14), kind=kOutput, calls=%fused_computation.19 | convolution fusion | flops 12891193344 | bytes 27262976 | tf_op jit(solution)/shard_map/dot_general | solution.py:90
  396.8 6.1 fusion.57
  402.9 19.1 %fusion.27 = f32[8,1024,1024]{2,1,0:T(8,128)} fusion(f32[1024,8,128]{0,2,1:T(8,128)} %copy-done.3, bf16[1024,1024]{1,0:T(8,128)(2,1)S(1)} %copy-done), kind=kOutput, calls=%fused_computation.36 | convolution fusion | flops 6442450944 | bytes 39845888 | tf_op jit(solution)/shard_map/thf,uhf->htu/dot_general | solution.py:119
  421.9 18.4 %fusion.15 = bf16[1024,8,128]{0,2,1:T(8,128)(2,1)} fusion(f32[8,128,1024]{2,1,0:T(8,128)} %fusion.57, bf16[1024,8,128]{0,2,1:T(8,128)(2,1)} %copy.37, f32[8,1024,1024]{2,1,0:T(8,128)} %fusion.27, f32[1024,1024]{1,0:T(8,128)S(1)} %copy-done.1, f32[1024]{0:T(1024)S(1)} %compare_convert_fusion.2), kind=kOutput, calls=%fused_computation.23 | convolution fusion | flops 6453985280 | bytes 46141440 | tf_op jit(solution)/shard_map/htu,uhe->the/dot_general | solution.py:128
  440.4 3.9 copy.54
  444.3 18.7 %fusion.6 = f32[8,128,1024]{2,1,0:T(8,128)} fusion(f32[1024,8,128]{0,2,1:T(8,128)} %copy-done.3, f32[8,1024,1024]{2,1,0:T(8,128)} %fusion.32, f32[1024,1024]{1,0:T(8,128)} %fusion.17), kind=kOutput, calls=%fused_computation.10 | convolution fusion | flops 6450839552 | bytes 46137344 | tf_op jit(solution)/shard_map/htu,thf->uhf/dot_general | solution.py:146
  463.1 31.1 %while.35 = (s32[]{:T(128)}, f32[1,1,1]{2,1,0:T(1,128)}, f32[8,128,128]{2,1,0:T(8,128)S(1)}, s32[]{:T(128)}, bf16[8,1,1,1]{0,3,2,1:T(2,128)(2,1)S(1)}, /*index=5...) while((s32[]{:T(128)}, f32[1,1,1]{2,1,0:T(1,128)}, ...), condition=%wide.region_6.7_spmd.clone, body=%wide.region_5.6_spmd.clone.sunk | while | flops 655373 | bytes 1310949 | solution.py:37
  465.0 1.3 fusion.85
  468.8 1.3 fusion.85
  472.7 1.3 fusion.85
  476.6 1.3 fusion.85
  480.5 1.3 fusion.85
  484.4 1.3 fusion.85
  488.2 1.3 fusion.85
  492.1 1.3 fusion.85
  494.2 5.7 add_convert_fusion
  499.9 3.9 copy.56
  503.8 1.3 fusion.25
  506.7 17.2 %fusion.14 = bf16[1024,8,128]{0,2,1:T(8,128)(2,1)} fusion(f32[8,128,1024]{2,1,0:T(8,128)S(1)} %fusion.25, bf16[1024,8,128]{0,2,1:T(8,128)(2,1)S(1)} %bitcast.135, f32[8,1024,1024]{2,1,0:T(8,128)} %fusion.27, f32[1024,1024]{1,0:T(8,128)S(1)} %copy-done.2, f32[1024]{0:T(1024)S(1)} %compare_convert_fusion), kind=kOutput, calls=%fused_computation.21 | convolution fusion | flops 6453985280 | bytes 46141440 | tf_op jit(solution)/shard_map/htu,the->uhe/dot_general | solution.py:133
  523.9 3.9 copy.55
  527.9 3.3 convert_element_type.140
  531.2 148.1 %reduce-scatter.3.cloned.1.call-done = bf16[1024,1536]{1,0:T(8,128)(2,1)} async-done(((bf16[1024,6144]{1,0:T(8,128)(2,1)}), bf16[1024,1536]{1,0:T(8,128)(2,1)}) %reduce-scatter.3.cloned.1.call-update) | async-done | bytes 3145744 | tf_op jit(solution)/shard_map/reduce_scatter | solution.py:91
  (74 shorter events, 20.9 us)
Async XLA Ops:
  7.2 10.4 %copy-start = (bf16[1024,1024]{1,0:T(8,128)(2,1)S(1)}, bf16[1024,1024]{1,0:T(8,128)(2,1)}, u32[]{:S(2)}) copy-start(bf16[1024,1024]{1,0:T(8,128)(2,1)} %param.12) | copy-start | bytes 6291460
  7.2 57.4 %all-gather.9.cloned.1.call-start = ((), (), s32[]{:S(2)}) async-start(), calls=%async_computation.4 | async-start | bytes 2359296 | tf_op jit(solution)/shard_map/all_gather | solution.py:19
  8.6 7.7 %copy-start.11 = (s32[1024]{0:T(1024)S(1)}, s32[1024]{0:T(1024)}, u32[]{:S(2)}) copy-start(s32[1024]{0:T(1024)} %param.13) | copy-start | bytes 12292
  17.6 3.9 copy-start.14
  20.7 250.6 %all-gather.11.cloned.1.call-start = ((), (), s32[]{:S(2)}) async-start(), calls=%async_computation.5 | async-start | bytes 15728640 | tf_op jit(solution)/shard_map/all_gather | solution.py:12
  21.5 441.5 %all-gather.13.cloned.1.call-start = ((), (), s32[]{:S(2)}) async-start(), calls=%async_computation.6 | async-start | bytes 2359296 | tf_op jit(solution)/shard_map/all_gather | solution.py:19
  45.8 2.8 copy-start.4
  45.8 3.8 copy-start.7
  312.3 21.5 %copy-start.8 = (f32[1024,8,128]{0,2,1:T(8,128)S(1)}, f32[1024,8,128]{0,2,1:T(8,128)}, u32[]{:S(2)}) copy-start(f32[1024,8,128]{0,2,1:T(8,128)} %get-tuple-element.387) | copy-start | bytes 12582916
  333.8 4.9 copy-start.5
  336.8 2.0 copy-start.3
  340.8 187.1 %reduce-scatter.5.cloned.1.call-start = ((), (), s32[]{:S(2)}) async-start(), calls=%async_computation.3 | async-start | bytes 14155776 | tf_op jit(solution)/shard_map/reduce_scatter | solution.py:101
  340.9 13.1 %copy-start.10 = (bf16[1024,8,128]{0,2,1:T(8,128)(2,1)S(1)}, bf16[1024,8,128]{0,2,1:T(8,128)(2,1)}, u32[]{:S(2)}) copy-start(bf16[1024,8,128]{0,2,1:T(8,128)(2,1)} %get-tuple-element.379) | copy-start | bytes 6291460
  374.3 304.9 %reduce-scatter.3.cloned.1.call-start = ((), (), s32[]{:S(2)}) async-start(), calls=%async_computation.2 | async-start | bytes 15728640 | tf_op jit(solution)/shard_map/reduce_scatter | solution.py:91
  402.9 19.1 %copy-start.1 = (f32[1024,1024]{1,0:T(8,128)S(1)}, f32[1024,1024]{1,0:T(8,128)}, u32[]{:S(2)}) copy-start(f32[1024,1024]{1,0:T(8,128)} %fusion.17) | copy-start | bytes 12582916
  444.3 18.8 %copy-start.9 = (f32[8,128,128]{2,1,0:T(8,128)S(1)}, f32[8,128,128]{2,1,0:T(8,128)}, u32[]{:S(2)}) copy-start(f32[8,128,128]{2,1,0:T(8,128)} %custom-call.1) | copy-start | bytes 1572868
  444.3 18.8 %copy-start.13 = (bf16[8]{0:T(256)(128)(2,1)S(1)}, bf16[8]{0:T(256)(128)(2,1)}, u32[]{:S(2)}) copy-start(bf16[8]{0:T(256)(128)(2,1)} %get-tuple-element.375) | copy-start | bytes 52
  463.0 31.2 %copy-start.12 = (s32[1024]{0:T(1024)S(1)}, s32[1024]{0:T(1024)}, u32[]{:S(2)}) copy-start(s32[1024]{0:T(1024)} %param.13) | copy-start | bytes 12292
  503.8 2.2 copy-start.2
  503.8 2.9 copy-start.6
Sparse Core Ops, SparseCore 0:
  20.9 30.6 all-gather.8
  53.1 218.1 all-gather.10
  341.0 25.9 all-gather.12
  374.5 90.0 reduce-scatter.4
  467.3 211.9 reduce-scatter.2
